TPU v7x, 32 devices: a whole 2x2x4 slice. The times are simulated.
32 devices in a mesh: expert: 16 (over z, y, core), tensor: 2 (over x).
Axes of the slice: x: 2, y: 2, z: 4, core: 2. Of those that a mesh axis runs over, the one named last changes fastest.
Arguments:
- tokens: bfloat16 [4096, 2560], P(('expert', 'tensor')), may hold values from -6 to 6
- expert_ids: int32 [4096, 1], P(('expert', 'tensor')), may hold values from 0 to 7; in each aligned block of 128 rows (0 to 127, 128 to 255, ...) at most 24 rows name the same one
- gate_weights: bfloat16 [4096, 1], P(('expert', 'tensor')), may hold values from 0.19921875 to 1
- routed_up: bfloat16 [16, 2560, 2048], P('expert', None, 'tensor'), may hold values from -0.125 to 0.125
- routed_down: bfloat16 [16, 2048, 2560], P('expert', 'tensor'), may hold values from -0.09375 to 0.09375
- shared_up: bfloat16 [2560, 4096], P('expert', 'tensor'), may hold values from -0.125 to 0.125
- shared_down: bfloat16 [4096, 2560], P('tensor', 'expert'), may hold values from -0.09375 to 0.09375
Outputs:
- layer_out: bfloat16 [4096, 2560], P(('expert', 'tensor'))
Inputs may be any that keep to these rules, and one draw needn't show every extreme that they name: `expert_ids`: each token names one of 8 experts; among the 128 tokens of one device at most 24 name the same expert, and in every draw some device's tokens name one expert exactly 24 times.
All inputs are finite; a program needn't handle non-finite values.
Results may differ from a plain program's by a relative error of at most 0.0073.
Values may be sent and summed in bfloat16 or wider, within the bound.
A program may use at most 128 MiB of HBM per device.

v0:
```python
import jax
import jax.numpy as jnp
from jax import lax
from jax.sharding import PartitionSpec as P


def place_matrix(route_ids, experts, capacity):
    columns = jnp.arange(experts, dtype=jnp.int32)
    onehot = (route_ids[:, None] == columns[None, :]).astype(jnp.int32)
    before = jnp.cumsum(onehot, axis=0) - onehot
    rank_of = jnp.sum(before * onehot, axis=1)
    target = route_ids * capacity + rank_of
    slots_all = jnp.arange(experts * capacity, dtype=jnp.int32)
    return (slots_all[:, None] == target[None, :]).astype(jnp.bfloat16)


def on_device(tokens, expert_ids, gate_weights, routed_up, routed_down, shared_up, shared_down):
    width = tokens.shape[1]
    tok_rows = tokens.shape[0]
    n_expert = lax.axis_size("expert")
    n_tensor = lax.axis_size("tensor")
    experts = n_expert // 2
    capacity = max(2, 3 * tok_rows // (2 * experts))
    everyone, all_ids = (
        lax.all_gather(tokens, "tensor", axis=0, tiled=True),
        lax.all_gather(expert_ids, "tensor", axis=0, tiled=True),
    )
    shared_acc = jnp.dot(
        everyone,
        lax.all_gather(shared_up, "expert", axis=0, tiled=True),
        preferred_element_type=jnp.float32,
    )
    shared_hidden = jax.nn.silu(shared_acc).astype(jnp.bfloat16)
    shared_part = jnp.dot(
        shared_hidden,
        lax.all_gather(shared_down, "expert", axis=1, tiled=True),
        preferred_element_type=jnp.float32,
    )
    own_place = place_matrix(expert_ids[:, 0], experts, capacity)
    packed = jnp.dot(own_place, tokens, preferred_element_type=jnp.float32).astype(jnp.bfloat16)
    own = packed.reshape(experts, 1, capacity, width)
    own = jnp.broadcast_to(own[:, None], (experts, 2, 1, capacity, width)).reshape(
        n_expert, 1, capacity, width
    )
    mine = lax.all_to_all(own, "expert", split_axis=0, concat_axis=0, tiled=True)
    arrived = lax.all_gather(mine, "tensor", axis=1, tiled=True)
    flat = arrived.reshape(-1, width)
    hidden = jax.nn.silu(jnp.dot(flat, routed_up[0], preferred_element_type=jnp.float32)).astype(
        jnp.bfloat16
    )
    partial_out = jnp.dot(hidden, routed_down[0], preferred_element_type=jnp.float32)
    shaped = partial_out.reshape(n_expert, n_tensor, capacity, width)
    summed = lax.psum_scatter(shaped, "tensor", scatter_dimension=1, tiled=True)
    returned = lax.all_to_all(
        summed.astype(jnp.bfloat16), "expert", split_axis=0, concat_axis=0, tiled=True
    )
    paired = returned.reshape(experts, 2, capacity, width)
    routed = jnp.einsum(
        "st,sd->td",
        own_place,
        paired[:, 0].reshape(experts * capacity, width),
        preferred_element_type=jnp.float32,
    )
    routed = routed + jnp.einsum(
        "st,sd->td",
        own_place,
        paired[:, 1].reshape(experts * capacity, width),
        preferred_element_type=jnp.float32,
    )
    routed = gate_weights.astype(jnp.float32) * routed
    shared_own = lax.psum_scatter(shared_part, "tensor", scatter_dimension=0, tiled=True)
    return (routed + shared_own).astype(jnp.bfloat16)


def solution(mesh):
    placed = (
        P(("expert", "tensor"), None),
        P(("expert", "tensor"), None),
        P(("expert", "tensor"), None),
        P("expert", None, "tensor"),
        P("expert", "tensor", None),
        P("expert", "tensor"),
        P("tensor", "expert"),
    )
    return jax.shard_map(
        on_device,
        mesh=mesh,
        in_specs=placed,
        out_specs=P(("expert", "tensor"), None),
        check_vma=False,
    )
```

profile of v0, /device:TPU:13, one launch (start us, length us, event | category | flops | bytes accessed | tf_op | source)
XLA Modules:
  0.0 607.3 jit_solution(7669185050274071382)
XLA Ops:
  6.5 0.0 all-gather.5.cloned.1.call-start
  6.5 0.7 fusion.12
  7.3 0.2 reduce_window_sum.11
  7.5 0.8 select_reduce_fusion
  8.3 0.7 multiply_add_fusion
  9.0 1.5 convolution_convert_fusion
  10.4 0.1 broadcast_in_dim.13
  10.6 50.9 %all_to_all.10 = bf16[16,1,24,2560]{3,2,1,0:T(8,128)(2,1)} all-to-all(bf16[16,1,24,2560]{3,2,1,0:T(8,128)(2,1)S(1)} %bitcast.36), channel_id=1, replica_groups=mesh['expert'=16,'tensor'=2] {'expert'}, dimensions={0} | all-to-all | bytes 3932160 | tf_op jit(solution)/shard_map/all_to_all | solution.py:45
  61.5 0.0 copy-start.1
  61.5 0.0 all-gather.5.cloned.1.call-update
  61.5 0.0 all-gather.7.cloned.1.call-start
  61.6 0.7 all-gather.7.cloned.1.call-update
  62.3 0.0 all-gather.11.cloned.1.call-start
  62.3 0.7 all-gather.11.cloned.1.call-update
  63.0 0.0 all-gather.9.cloned.1.call-start
  63.0 0.0 slice-start
  63.1 0.5 all-gather.9.cloned.1.call-update
  63.6 0.0 reduce-scatter.3.cloned.1.call-start
  63.6 0.0 copy-done.1
  63.6 0.6 dynamic-slice
  64.2 50.7 %all-gather.5.cloned.1.call-done = bf16[16,2,24,2560]{3,2,1,0:T(8,128)(2,1)} async-done(((bf16[16,1,24,2560]{3,2,1,0:T(8,128)(2,1)}), bf16[16,2,24,2560]{3,2,1,0:T(8,128)(2,1)}) %all-gather.5.cloned.1.call-update) | async-done | bytes 3932176 | tf_op jit(solution)/shard_map/all_gather | solution.py:46
  114.9 0.0 slice-start.1
  114.9 8.4 %multiply_convert_fusion = bf16[768,1024]{1,0:T(8,128)(2,1)S(1)} fusion(bf16[768,2560]{1,0:T(8,128)(2,1)} %bitcast.44, bf16[1,2560,1024]{2,1,0:T(8,128)(2,1)} %param.10), kind=kOutput, calls=%fused_computation.10 | convolution fusion | flops 4030464000 | bytes 10747904 | tf_op jit(solution)/shard_map/dot_general | solution.py:48
  123.3 0.0 slice-done
  123.3 0.0 slice-done.1
  123.3 6.4 %fusion = f32[16,2,24,2560]{3,2,1,0:T(8,128)} fusion(bf16[16,2,24,1024]{3,2,1,0:T(8,128)(2,1)S(1)} %bitcast.45, bf16[1,1024,2560]{2,1,0:T(8,128)(2,1)S(1)} %bitcast.43), kind=kOutput, calls=%fused_computation | convolution fusion | flops 4026531840 | bytes 14680064 | tf_op jit(solution)/shard_map/dot_general | solution.py:51
  129.7 11.0 %all-gather.7.cloned.1.call-done = bf16[256,2560]{1,0:T(8,128)(2,1)} async-done(((bf16[128,2560]{1,0:T(8,128)(2,1)}), bf16[256,2560]{1,0:T(8,128)(2,1)}) %all-gather.7.cloned.1.call-update) | async-done | bytes 1310736 | tf_op jit(solution)/shard_map/all_gather | solution.py:25
  140.7 88.7 %all-gather.11.cloned.1.call-done = bf16[2048,2560]{0,1:T(8,128)(2,1)} async-done(((bf16[2048,160]{0,1:T(8,128)(2,1)}), bf16[2048,2560]{0,1:T(8,128)(2,1)}) %all-gather.11.cloned.1.call-update) | async-done | bytes 10485776 | tf_op jit(solution)/shard_map/all_gather | solution.py:36
  229.4 87.9 %all-gather.9.cloned.1.call-done = bf16[2560,2048]{1,0:T(8,128)(2,1)} async-done(((bf16[160,2048]{1,0:T(8,128)(2,1)}), bf16[2560,2048]{1,0:T(8,128)(2,1)}) %all-gather.9.cloned.1.call-update) | async-done | bytes 10485776 | tf_op jit(solution)/shard_map/all_gather | solution.py:30
  317.4 14.5 %fusion.9 = f32[256,2560]{1,0:T(8,128)} fusion(bf16[2048,2560]{0,1:T(8,128)(2,1)} %all-gather.11.cloned.1.call-done, bf16[256,2560]{1,0:T(8,128)(2,1)} %all-gather.7.cloned.1.call-done, bf16[2560,2048]{1,0:T(8,128)(2,1)} %all-gather.9.cloned.1.call-done), kind=kOutput, calls=%fused_computation.12 | convolution fusion | flops 5371330560 | bytes 24903680 | tf_op jit(solution)/shard_map/dot_general | solution.py:34
  331.9 0.0 reduce-scatter.3.cloned.1.call-update
  331.9 211.0 %all-reduce.2 = bf16[16,2,24,2560]{3,2,1,0:T(8,128)(2,1)} all-reduce(f32[16,2,24,2560]{3,2,1,0:T(8,128)} %fusion), channel_id=2, replica_groups=mesh['expert'=16,'tensor'=2] {'tensor'}, use_global_device_ids=true, to_apply=%region_2.3.clone | all-reduce | flops 1966080 | bytes 11796480
  542.9 3.6 dynamic-slice_convert_fusion
  546.5 0.0 copy-start
  546.5 6.5 %all-to-all-start.1 = ((bf16[16,1,24,2560]{3,2,1,0:T(8,128)(2,1)}), bf16[16,1,24,2560]{3,2,1,0:T(8,128)(2,1)S(1)}, u32[]{:S(2)}, u32[]{:S(2)}) async-start(bf16[16,1,24,2560]{3,2,1,0:T(8,128)(2,1)} %dynamic-slice_convert_fusion), calls=%async_computation.1 | async-start | bytes 3932160 | tf_op jit(solution)/shard_map/all_to_all | solution.py:54
  553.0 0.0 copy-done
  553.0 44.6 %all-to-all-done.1 = bf16[16,1,24,2560]{3,2,1,0:T(8,128)(2,1)S(1)} async-done(((bf16[16,1,24,2560]{3,2,1,0:T(8,128)(2,1)}), bf16[16,1,24,2560]{3,2,1,0:T(8,128)(2,1)S(1)}, u32[]{:S(2)}, u32[]{:S(2)}) %all-to-all-start.1) | async-done | bytes 1966112 | tf_op jit(solution)/shard_map/all_to_all | solution.py:54
  597.6 0.1 fusion.17
  597.8 0.4 fusion.11
  598.1 0.0 reduce-scatter.3.cloned.1.call-done
  598.2 2.6 fusion.6
  (2 shorter events, 0.0 us)
Async XLA Ops:
  6.5 108.4 %all-gather.5.cloned.1.call-start = ((), (), s32[]{:S(2)}) async-start(), calls=%async_computation.3 | async-start | bytes 5898240 | tf_op jit(solution)/shard_map/all_gather | solution.py:46
  61.5 2.1 copy-start.1
  61.5 79.2 %all-gather.7.cloned.1.call-start = ((), (), s32[]{:S(2)}) async-start(), calls=%async_computation.4 | async-start | bytes 1966080 | tf_op jit(solution)/shard_map/all_gather | solution.py:25
  62.3 167.2 %all-gather.11.cloned.1.call-start = ((), (), s32[]{:S(2)}) async-start(), calls=%async_computation.6 | async-start | bytes 11141120 | tf_op jit(solution)/shard_map/all_gather | solution.py:36
  63.0 254.4 %all-gather.9.cloned.1.call-start = ((), (), s32[]{:S(2)}) async-start(), calls=%async_computation.5 | async-start | bytes 11141120 | tf_op jit(solution)/shard_map/all_gather | solution.py:30
  63.0 60.2 %slice-start = ((s8[5242880]{0:T(1024)(128)(4,1)}), s8[1048576]{0:T(1024)(128)(4,1)S(1)}, s32[]{:S(2)}) async-start(s8[5242880]{0:T(1024)(128)(4,1)} %bitcast.42), calls=%async_computation.8 | async-start | bytes 2097152
  63.6 534.6 %reduce-scatter.3.cloned.1.call-start = ((), (), s32[]{:S(2)}) async-start(), calls=%async_computation.7 | async-start | bytes 3932160 | tf_op jit(solution)/shard_map/reduce_scatter | solution.py:71
  114.9 8.4 %slice-start.1 = ((s8[5242880]{0:T(1024)(128)(4,1)}), s8[4194304]{0:T(1024)(128)(4,1)S(1)}, s32[]{:S(2)}) async-start(s8[5242880]{0:T(1024)(128)(4,1)} %bitcast.42), calls=%async_computation.9 | async-start | bytes 8388608
  546.5 6.5 %copy-start = (bf16[128,1]{0,1:T(2,128)(2,1)S(1)}, bf16[128,1]{0,1:T(2,128)(2,1)}, u32[]{:S(2)}) copy-start(bf16[128,1]{0,1:T(2,128)(2,1)} %param.9) | copy-start | bytes 772
  546.5 51.1 %all-to-all-start.1 = ((bf16[16,1,24,2560]{3,2,1,0:T(8,128)(2,1)}), bf16[16,1,24,2560]{3,2,1,0:T(8,128)(2,1)S(1)}, u32[]{:S(2)}, u32[]{:S(2)}) async-start(bf16[16,1,24,2560]{3,2,1,0:T(8,128)(2,1)} %dynamic-slice_convert_fusion), calls=%async_computation.1 | async-start | bytes 3932160 | tf_op jit(solution)/shard_map/all_to_all | solution.py:54
Sparse Core Ops, SparseCore 0:
  61.6 53.2 all-gather.4
  116.4 24.2 all-gather.6
  143.0 86.4 all-gather.10
  231.6 85.7 all-gather.8
  332.0 65.2 reduce-scatter.2
where the time goes:
time: 608 us; the launch traced here: 607 us
  waiting for transfers between devices  285 us (47%)
  blocking collectives  262 us (43%)
  matrix products  33.7 us (6%)
  between operations  13.3 us (2%)
  starting transfers between devices  6.63 us (1%)
    unnamed x1, blocking collectives  211 us
    all_gather x1, waiting for transfers between devices, on_device(): lax.all_gather(shared_down, 'expert', axis=1, tiled=True)  88.7 us
    all_gather x1, waiting for transfers between devices, on_device(): lax.all_gather(shared_up, 'expert', axis=0, tiled=True)  87.9 us
    all_to_all x1, blocking collectives, on_device(): lax.all_to_all(own, 'expert', split_axis=0, concat_axis=0, tiled=True)  50.9 us
    all_gather x1, waiting for transfers between devices, on_device(): arrived = lax.all_gather(mine, 'tensor', axis=1, tiled=True)  50.7 us
    all_to_all x1, waiting for transfers between devices, on_device(): lax.all_to_all(summed.astype(jnp.bfloat16), 'expert', split_axis=0, conca...  44.6 us
    dot_general x1, matrix products, on_device(): jnp.dot(shared_hidden, lax.all_gather(shared_down, 'expert', axis=1, tile...  14.5 us
  transfers between devices with their start and end apart: 6, of which 5 were waited for; matrix products, arithmetic and copies ran while one was open for 3% of the time, Pallas kernels for 0%

commit v1 on v0

v1 whole, which is shorter than its diff:
```python
import functools

import jax
import jax.numpy as jnp
from jax import lax
from jax.experimental import pallas as pl
from jax.experimental.pallas import tpu as pltpu
from jax.sharding import PartitionSpec as P

MESH = pl.DeviceIdType.MESH


def place_matrix(route_ids, experts, capacity):
    columns = jnp.arange(experts, dtype=jnp.int32)
    onehot = (route_ids[:, None] == columns[None, :]).astype(jnp.int32)
    before = jnp.cumsum(onehot, axis=0) - onehot
    rank_of = jnp.sum(before * onehot, axis=1)
    target = route_ids * capacity + rank_of
    slots_all = jnp.arange(experts * capacity, dtype=jnp.int32)
    return (slots_all[:, None] == target[None, :]).astype(jnp.bfloat16)


class Place:
    def __init__(self, chips):
        me = lax.axis_index("expert")
        self.chips = chips
        self.x = lax.axis_index("tensor")
        self.chip = me // 2
        self.core = me % 2
        odd = self.chip % 2
        self.pos = (1 - odd) * (self.chip // 2) + odd * (chips - 1 - self.chip // 2)

    def chip_at(self, pos):
        pos = (pos + self.chips) % self.chips
        high = pos // (self.chips // 2)
        return (1 - high) * 2 * pos + high * (2 * (self.chips - 1 - pos) + 1)

    def peer(self, chip):
        return {"expert": chip * 2 + self.core, "tensor": self.x}

    def partner(self):
        return {"expert": self.chip * 2 + 1 - self.core, "tensor": self.x}

    def across(self):
        return {"expert": self.chip * 2 + self.core, "tensor": 1 - self.x}


def greet(place):
    barrier = pltpu.get_barrier_semaphore()

    def one(step, carry):
        peer = place.peer((place.chip + step) % place.chips)
        pl.semaphore_signal(barrier, inc=1, device_id=peer, device_id_type=MESH)
        return carry

    lax.fori_loop(1, place.chips, one, 0)
    pl.semaphore_signal(barrier, inc=1, device_id=place.partner(), device_id_type=MESH)
    pl.semaphore_signal(barrier, inc=1, device_id=place.across(), device_id_type=MESH)
    pl.semaphore_wait(barrier, place.chips + 1)


def send(src, dst, sends, recvs, k, device):
    copy = pltpu.make_async_remote_copy(
        src_ref=src,
        dst_ref=dst,
        send_sem=sends.at[k],
        recv_sem=recvs.at[k],
        device_id=device,
        device_id_type=MESH,
    )
    copy.start()
    return copy


class Ring:
    def __init__(self, place, block, whole, sems):
        self.place, self.block, self.whole = place, block, whole
        self.fs, self.fr, self.bs, self.br, self.ps, self.pr, self.own = sems
        self.forward = place.chips // 2
        self.backward = place.chips - 1 - self.forward
        self.fcopies, self.bcopies, self.pcopies = [], [], []

    def slot(self, pos):
        return self.whole.at[self.place.chip_at(pos) * 2 + self.place.core]

    def hop(self, s, ahead):
        place = self.place
        pos = place.pos - s if ahead else place.pos + s
        src = self.block if s == 0 else self.slot(pos)
        if ahead and s < self.forward:
            device = place.peer(place.chip_at(place.pos + 1))
            self.fcopies.append(send(src, self.slot(pos), self.fs, self.fr, s, device))
        if not ahead and s < self.backward:
            device = place.peer(place.chip_at(place.pos - 1))
            self.bcopies.append(send(src, self.slot(pos), self.bs, self.br, s, device))
        if ahead or s > 0:
            k = s if ahead else self.forward + s
            self.pcopies.append(send(src, self.slot(pos), self.ps, self.pr, k, place.partner()))

    def start(self):
        self.hop(0, True)
        self.hop(0, False)
        self.local = pltpu.make_async_copy(self.block, self.slot(self.place.pos), self.own)
        self.local.start()

    def step(self, s):
        self.fcopies[s - 1].wait_recv()
        self.hop(s, True)
        if s <= self.backward:
            self.bcopies[s - 1].wait_recv()
            self.hop(s, False)

    def finish(self):
        self.local.wait()
        for copy in self.fcopies + self.bcopies:
            copy.wait_send()
        for copy in self.pcopies:
            copy.wait()


def ring_sems(chips):
    forward = chips // 2
    backward = max(1, chips - 1 - forward)
    dma = pltpu.SemaphoreType.DMA
    return [
        dma((forward,)),
        dma((forward,)),
        dma((backward,)),
        dma((backward,)),
        dma((chips,)),
        dma((chips,)),
        dma,
    ]


def first_kernel(chips, packed, tokens, block, arrived, other, whole, *sems):
    ring_part, (ds, dr, gs, gr, local_sem) = sems[:7], sems[7:]
    place = Place(chips)
    greet(place)
    mine = arrived.at[place.x * 2 + place.core]
    local = pltpu.make_async_copy(packed.at[place.chip], mine.at[place.chip], local_sem)
    local.start()
    dispatch = []
    for step in range(1, chips):
        chip = (place.chip + step) % chips
        dispatch.append(
            send(packed.at[chip], mine.at[place.chip], ds, dr, step, place.peer(chip))
        )
    shared = send(tokens, other, gs, gr, 0, place.across())
    ring = Ring(place, block, whole, ring_part)
    ring.start()
    local.wait()
    for copy in dispatch:
        copy.wait_recv()
    over = send(mine, mine, gs, gr, 1, place.across())
    near = send(mine, mine, gs, gr, 2, place.partner())
    last = ring.forward
    for s in range(1, last):
        ring.step(s)
    over.wait_recv()
    far = arrived.at[(1 - place.x) * 2 + place.core]
    relay = send(far, far, gs, gr, 3, place.partner())
    ring.step(last)
    ring.finish()
    for copy in dispatch:
        copy.wait_send()
    over.wait_send()
    shared.wait()
    near.wait()
    relay.wait()


def second_kernel(chips, partial, block, returned, whole, swap, cross, ours, total, *sems):
    ring_part, (rs, rr, gs, gr, local_sem) = sems[:7], sems[7:]
    place = Place(chips)
    greet(place)
    swaps = []
    for t in range(2):
        group = (1 - place.x) if t == 0 else place.x
        src = partial.at[group * 2 + 1 - place.core]
        swaps.append(send(src, swap.at[t], gs, gr, t, place.partner()))
    ring = Ring(place, block, whole, ring_part)
    ring.start()

    def add(first, second, out):
        def one(i, carry):
            out[i] = (first[i].astype(jnp.float32) + second[i].astype(jnp.float32)).astype(
                jnp.bfloat16
            )
            return carry

        lax.fori_loop(0, chips, one, 0)

    swaps[0].wait_recv()
    add(partial.at[(1 - place.x) * 2 + place.core], swap.at[0], ours)
    over = send(ours, cross, gs, gr, 2, place.across())
    swaps[1].wait_recv()
    own = partial.at[place.x * 2 + place.core]
    mid = ring.forward // 2
    for s in range(1, mid + 1):
        ring.step(s)
    over.wait_recv()

    def three(i, carry):
        total[i] = (
            own[i].astype(jnp.float32)
            + swap[1, i].astype(jnp.float32)
            + cross[i].astype(jnp.float32)
        ).astype(jnp.bfloat16)
        return carry

    lax.fori_loop(0, chips, three, 0)
    local = pltpu.make_async_copy(total.at[place.chip], returned.at[place.chip], local_sem)
    local.start()
    back = []
    for step in range(1, chips):
        chip = (place.chip + step) % chips
        back.append(send(total.at[chip], returned.at[place.chip], rs, rr, step, place.peer(chip)))
    for s in range(mid + 1, ring.forward + 1):
        ring.step(s)
    ring.finish()
    local.wait()
    for copy in back:
        copy.wait()
    over.wait_send()
    swaps[0].wait_send()
    swaps[1].wait_send()


def on_device(tokens, expert_ids, gate_weights, routed_up, routed_down, shared_up, shared_down):
    tok_rows, width = tokens.shape
    n_expert = lax.axis_size("expert")
    chips = n_expert // 2
    experts = chips
    capacity = max(2, 3 * tok_rows // (2 * experts))
    capacity = -(-capacity // 8) * 8
    rows, part = shared_up.shape
    bf16 = jnp.bfloat16
    hbm = pl.BlockSpec(memory_space=pl.ANY)
    vmem = pl.BlockSpec(memory_space=pltpu.VMEM)
    dma = pltpu.SemaphoreType.DMA
    down_rows = shared_down.T

    own_place = place_matrix(expert_ids[:, 0], experts, capacity)
    packed = jnp.dot(own_place, tokens, preferred_element_type=jnp.float32).astype(bf16)
    arrived, other, up = pl.pallas_call(
        functools.partial(first_kernel, chips),
        out_shape=[
            jax.ShapeDtypeStruct((4, chips, capacity, width), bf16),
            jax.ShapeDtypeStruct((tok_rows, width), bf16),
            jax.ShapeDtypeStruct((n_expert, rows, part), bf16),
        ],
        in_specs=[vmem] * 3,
        out_specs=[hbm] * 3,
        scratch_shapes=ring_sems(chips)
        + [dma((chips,)), dma((chips,)), dma((4,)), dma((4,)), dma],
        compiler_params=pltpu.CompilerParams(collective_id=1, has_side_effects=True),
        name="gather_up_and_dispatch",
    )(packed.reshape(experts, capacity, width), tokens, shared_up)

    flat = arrived.reshape(-1, width)
    hidden = jax.nn.silu(jnp.dot(flat, routed_up[0], preferred_element_type=jnp.float32)).astype(
        bf16
    )
    partial = jnp.dot(hidden, routed_down[0], preferred_element_type=jnp.float32).astype(bf16)
    returned, down = pl.pallas_call(
        functools.partial(second_kernel, chips),
        out_shape=[
            jax.ShapeDtypeStruct((chips, capacity, width), bf16),
            jax.ShapeDtypeStruct((n_expert, rows, part), bf16),
        ],
        in_specs=[vmem] * 2,
        out_specs=[hbm] * 2,
        scratch_shapes=[
            pltpu.VMEM((2, chips, capacity, width), bf16),
            pltpu.VMEM((chips, capacity, width), bf16),
            pltpu.VMEM((chips, capacity, width), bf16),
            pltpu.VMEM((chips, capacity, width), bf16),
        ]
        + ring_sems(chips)
        + [dma((chips,)), dma((chips,)), dma((3,)), dma((3,)), dma],
        compiler_params=pltpu.CompilerParams(
            collective_id=2, has_side_effects=True, vmem_limit_bytes=60 * 1024 * 1024
        ),
        name="gather_down_and_return",
    )(partial.reshape(4, chips, capacity, width), down_rows)

    both = jnp.concatenate([tokens, other], axis=0)
    shared_acc = jnp.dot(both, up.reshape(n_expert * rows, part), preferred_element_type=jnp.float32)
    shared_hidden = jax.nn.silu(shared_acc).astype(bf16)
    shared_part = lax.dot_general(
        shared_hidden,
        down.reshape(n_expert * rows, part),
        (((1,), (1,)), ((), ())),
        preferred_element_type=jnp.float32,
    )
    theirs = lax.ppermute(shared_part[tok_rows:].astype(bf16), "tensor", [(0, 1), (1, 0)])
    routed = jnp.einsum(
        "st,sd->td",
        own_place,
        returned.reshape(experts * capacity, width),
        preferred_element_type=jnp.float32,
    )
    routed = gate_weights.astype(jnp.float32) * routed
    return (routed + shared_part[:tok_rows] + theirs.astype(jnp.float32)).astype(bf16)


def solution(mesh):
    placed = (
        P(("expert", "tensor"), None),
        P(("expert", "tensor"), None),
        P(("expert", "tensor"), None),
        P("expert", None, "tensor"),
        P("expert", "tensor", None),
        P("expert", "tensor"),
        P("tensor", "expert"),
    )
    return jax.shard_map(
        on_device,
        mesh=mesh,
        in_specs=placed,
        out_specs=P(("expert", "tensor"), None),
        check_vma=False,
    )
```

time: 608 us -> 229 us (0.38)
  waiting for transfers between devices: 285 us -> 15 us
  blocking collectives: 262 us -> 0 us
  Pallas kernels: 0 us -> 176 us
  between operations: 13.3 us -> 0.07 us
    all_gather x4 -> x0, waiting for transfers between devices: 238 us -> none  [the longest x1 88.7 us: on_device(): lax.all_gather(shared_down, 'expert', axis=1, tiled=True)]
    unnamed x1 -> x0, blocking collectives: 211 us -> none
    pallas_call x0 -> x2, Pallas kernels: none -> 176 us  [the longest x1 90.7 us: on_device(): pl.pallas_call(functools.partial(second_kernel, chips), out_shape=[jax.Sh...]
    all_to_all x1 -> x0, blocking collectives: 50.9 us -> none  [on_device(): lax.all_to_all(own, 'expert', split_axis=0, concat_axis=0, tiled=True)]
    all_to_all x1 -> x0, waiting for transfers between devices: 44.6 us -> none  [on_device(): lax.all_to_all(summed.astype(jnp.bfloat16), 'expert', split_axis=0, conca...]
    ppermute x0 -> x1, waiting for transfers between devices: none -> 15 us  [on_device(): lax.ppermute(shared_part[tok_rows:].astype(bf16), 'tensor', [(0, 1), (1,...]
    dot_general x5 -> x3, matrix products: 27.3 us -> 17.8 us  [the longest x1 12.9 us: on_device(): lax.dot_general(shared_hidden, down.reshape(n_expert * rows, part), (((1,...]
    dot_general x1, matrix products: 6.41 us -> 14.5 us  [on_device(): jnp.dot(hidden, routed_down[0], preferred_element_type=jnp.float32)]
  transfers between devices with their start and end apart: 6 -> 1, of which waited for: 5 -> 1; matrix products, arithmetic and copies ran while one was open for 3% -> 0% of each run, Pallas kernels for 0% -> 0%
where the time goes in v1:
time: 229 us; the launch traced here: 228 us
  Pallas kernels  176 us (77%)
  matrix products  32.3 us (14%)
  waiting for transfers between devices  15 us (7%)
  other arithmetic  2.4 us (1%)
    pallas_call x1, Pallas kernels, on_device(): pl.pallas_call(functools.partial(second_kernel, chips), out_shape=[jax.Sh...  90.7 us
    pallas_call x1, Pallas kernels, on_device(): pl.pallas_call(functools.partial(first_kernel, chips), out_shape=[jax.Sha...  85.7 us
    ppermute x1, waiting for transfers between devices, on_device(): lax.ppermute(shared_part[tok_rows:].astype(bf16), 'tensor', [(0, 1), (1,...  15 us
    dot_general x1, matrix products, on_device(): jnp.dot(hidden, routed_down[0], preferred_element_type=jnp.float32)  14.5 us
    dot_general x1, matrix products, on_device(): lax.dot_general(shared_hidden, down.reshape(n_expert * rows, part), (((1,...  12.9 us
  transfers between devices with their start and end apart: 1, of which 1 were waited for; matrix products, arithmetic and copies ran while one was open for 0% of the time, Pallas kernels for 0%

profile of v1, /device:TPU:13, one launch (start us, length us, event | category | flops | bytes accessed | tf_op | source)
XLA Modules:
  0.0 228.4 jit_solution(5367963655298632502)
XLA Ops:
  0.0 0.7 fusion.21
  0.7 0.2 reduce_window_sum.11
  0.9 0.8 select_reduce_fusion
  1.7 0.7 multiply_add_fusion
  2.4 2.4 %convolution_convert_fusion = bf16[192,2560]{1,0:T(8,128)(2,1)} fusion(bf16[128,2560]{1,0:T(8,128)(2,1)} %tokens.1, s32[128]{0:T(128)S(1)} %multiply_add_fusion), kind=kOutput, calls=%fused_computation.5 | convolution fusion | flops 126345216 | bytes 1638912 | tf_op jit(solution)/shard_map/dot_general | solution.py:245
  4.9 85.7 %gather_up_and_dispatch.1 = (bf16[4,8,24,2560]{3,2,1,0:T(8,128)(2,1)}, bf16[128,2560]{1,0:T(8,128)(2,1)}, bf16[16,160,2048]{2,1,0:T(8,128)(2,1)}) custom-call(bf16[8,24,2560]{2,1,0:T(8,128)(2,1)} %bitcast.30, bf16[128,2560]{1,0:T(8,128)(2,1)} %tokens.1, bf16[160,2048]{1,0:T(8,128)(2,1)} %block.1), custom_call_target="tpu_custom_call" | custom-call | tf_op jit(solution)/shard_map/gather_up_and_dispatch/pallas_call | solution.py:246
  90.6 14.5 %fusion.4 = bf16[768,2560]{1,0:T(8,128)(2,1)} fusion(bf16[1,1024,2560]{2,1,0:T(8,128)(2,1)} %param.11, bf16[768,2560]{1,0:T(8,128)(2,1)} %bitcast.37, bf16[1,2560,1024]{2,1,0:T(8,128)(2,1)} %param.10), kind=kOutput, calls=%fused_computation.4 | convolution fusion | flops 8058961920 | bytes 18350080 | tf_op jit(solution)/shard_map/dot_general | solution.py:265
  105.2 0.0 copy-start
  105.2 90.7 %gather_down_and_return.1 = (bf16[8,24,2560]{2,1,0:T(8,128)(2,1)}, bf16[16,160,2048]{2,1,0:T(8,128)(2,1)}) custom-call(bf16[4,8,24,2560]{3,2,1,0:T(8,128)(2,1)} %bitcast.29, bf16[160,2048]{1,0:T(8,128)(2,1)} %bitcast.32), custom_call_target="tpu_custom_call" | custom-call | tf_op jit(solution)/shard_map/gather_down_and_return/pallas_call | solution.py:266
  195.8 0.0 copy-done
  195.8 0.0 copy-start.1
  195.8 12.9 %fusion.19 = f32[256,2560]{1,0:T(8,128)S(1)} fusion(bf16[2560,2048]{1,0:T(8,128)(2,1)} %bitcast.36, bf16[2560,2048]{1,0:T(8,128)(2,1)} %bitcast.35, bf16[128,2560]{1,0:T(8,128)(2,1)} %get-tuple-element.12, bf16[128,2560]{1,0:T(8,128)(2,1)S(1)} %copy-done), kind=kOutput, calls=%fused_computation.16 | convolution fusion | flops 5373952000 | bytes 24903680 | tf_op jit(solution)/shard_map/dot_general | solution.py:291
  208.7 0.1 slice.15
  208.8 2.1 collective-permute-start
  210.9 0.0 copy-done.1
  210.9 15.0 %collective-permute-done = bf16[128,2560]{1,0:T(8,128)(2,1)S(1)} collective-permute-done((bf16[128,2560]{1,0:T(8,128)(2,1)S(1)}, bf16[128,2560]{1,0:T(8,128)(2,1)S(1)}, u32[]{:S(2)}, u32[]{:S(2)}) %collective-permute-start) | collective-permute-done | bytes 655392 | tf_op jit(solution)/shard_map/ppermute | solution.py:297
  225.9 2.5 %add_convert_fusion = bf16[128,2560]{1,0:T(8,128)(2,1)} fusion(bf16[128,2560]{1,0:T(8,128)(2,1)S(1)} %collective-permute-done, f32[256,2560]{1,0:T(8,128)S(1)} %fusion.19, bf16[192,2560]{1,0:T(8,128)(2,1)} %bitcast.31, f32[128]{0:T(128)S(1)} %bitcast_convert_fusion, s32[128]{0:T(128)S(1)} %multiply_add_fusion), kind=kOutput, calls=%fused_computation.15 | convolution fusion | flops 127492096 | bytes 3605504 | tf_op jit(solution)/shard_map/st,sd->td/dot_general | solution.py:298
  (1 shorter events, 0.0 us)
Async XLA Ops:
  105.2 90.7 %copy-start = (bf16[128,2560]{1,0:T(8,128)(2,1)S(1)}, bf16[128,2560]{1,0:T(8,128)(2,1)}, u32[]{:S(2)}) copy-start(bf16[128,2560]{1,0:T(8,128)(2,1)} %tokens.1) | copy-start | bytes 1966084
  195.8 15.1 %copy-start.1 = (bf16[128,1]{0,1:T(2,128)(2,1)S(1)}, bf16[128,1]{0,1:T(2,128)(2,1)}, u32[]{:S(2)}) copy-start(bf16[128,1]{0,1:T(2,128)(2,1)} %param.9) | copy-start | bytes 772
  208.8 17.1 %collective-permute-start = (bf16[128,2560]{1,0:T(8,128)(2,1)S(1)}, bf16[128,2560]{1,0:T(8,128)(2,1)S(1)}, u32[]{:S(2)}, u32[]{:S(2)}) collective-permute-start(bf16[128,2560]{1,0:T(8,128)(2,1)S(1)} %slice.15), channel_id=1, source_target_pairs={{0,1},{1,0},{2,3},{3,2},{4,5},{5,4},{6,7},{7,6},{8,9},{9,8},{10,11... | collective-permute-start | bytes 1966088 | tf_op jit(solution)/shard_map/ppermute | solution.py:297

commit v2 on v1

--- a/solution.py
+++ b/solution.py
@@ -73,15 +73,18 @@
 
 
 class Ring:
-    def __init__(self, place, block, whole, sems):
-        self.place, self.block, self.whole = place, block, whole
+    def __init__(self, place, block, whole, sems, piece, pieces):
+        rows = block.shape[0] // pieces
+        self.rows = pl.ds(piece * rows, rows)
+        self.place, self.block, self.whole = place, block.at[self.rows], whole
         self.fs, self.fr, self.bs, self.br, self.ps, self.pr, self.own = sems
-        self.forward = place.chips // 2
+        longer = place.chips // 2
+        self.forward = longer if piece == 0 else place.chips - 1 - longer
         self.backward = place.chips - 1 - self.forward
         self.fcopies, self.bcopies, self.pcopies = [], [], []
 
     def slot(self, pos):
-        return self.whole.at[self.place.chip_at(pos) * 2 + self.place.core]
+        return self.whole.at[self.place.chip_at(pos) * 2 + self.place.core, self.rows]
 
     def hop(self, s, ahead):
         place = self.place
@@ -103,12 +106,10 @@
         self.local = pltpu.make_async_copy(self.block, self.slot(self.place.pos), self.own)
         self.local.start()
 
-    def step(self, s):
-        self.fcopies[s - 1].wait_recv()
-        self.hop(s, True)
-        if s <= self.backward:
-            self.bcopies[s - 1].wait_recv()
-            self.hop(s, False)
+    def step(self, s, ahead):
+        if s <= (self.forward if ahead else self.backward):
+            (self.fcopies if ahead else self.bcopies)[s - 1].wait_recv()
+            self.hop(s, ahead)
 
     def finish(self):
         self.local.wait()
@@ -118,23 +119,43 @@
             copy.wait()
 
 
-def ring_sems(chips):
-    forward = chips // 2
-    backward = max(1, chips - 1 - forward)
+class Rings:
+    def __init__(self, place, block, whole, sems):
+        pieces = len(sems) // RING_SEMS
+        self.steps = place.chips // 2
+        self.rings = [
+            Ring(place, block, whole, sems[p * RING_SEMS : (p + 1) * RING_SEMS], p, pieces)
+            for p in range(pieces)
+        ]
+
+    def start(self):
+        for ring in self.rings:
+            ring.start()
+
+    def step(self, s):
+        for p in range(len(self.rings)):
+            self.rings[p].step(s, True)
+            self.rings[-1 - p].step(s, False)
+
+    def finish(self):
+        for ring in self.rings:
+            ring.finish()
+
+
+RING_SEMS = 7
+
+
+def pieces_of(rows):
+    return 2 if rows % 16 == 0 else 1
+
+
+def ring_sems(chips, pieces):
     dma = pltpu.SemaphoreType.DMA
-    return [
-        dma((forward,)),
-        dma((forward,)),
-        dma((backward,)),
-        dma((backward,)),
-        dma((chips,)),
-        dma((chips,)),
-        dma,
-    ]
+    return ([dma((chips // 2,))] * 4 + [dma((chips,)), dma((chips,)), dma]) * pieces
 
 
 def first_kernel(chips, packed, tokens, block, arrived, other, whole, *sems):
-    ring_part, (ds, dr, gs, gr, local_sem) = sems[:7], sems[7:]
+    ring_part, (ds, dr, gs, gr, local_sem) = sems[:-5], sems[-5:]
     place = Place(chips)
     greet(place)
     mine = arrived.at[place.x * 2 + place.core]
@@ -147,14 +168,14 @@
             send(packed.at[chip], mine.at[place.chip], ds, dr, step, place.peer(chip))
         )
     shared = send(tokens, other, gs, gr, 0, place.across())
-    ring = Ring(place, block, whole, ring_part)
+    ring = Rings(place, block, whole, ring_part)
     ring.start()
     local.wait()
     for copy in dispatch:
         copy.wait_recv()
     over = send(mine, mine, gs, gr, 1, place.across())
     near = send(mine, mine, gs, gr, 2, place.partner())
-    last = ring.forward
+    last = ring.steps
     for s in range(1, last):
         ring.step(s)
     over.wait_recv()
@@ -171,7 +192,7 @@
 
 
 def second_kernel(chips, partial, block, returned, whole, swap, cross, ours, total, *sems):
-    ring_part, (rs, rr, gs, gr, local_sem) = sems[:7], sems[7:]
+    ring_part, (rs, rr, gs, gr, local_sem) = sems[:-5], sems[-5:]
     place = Place(chips)
     greet(place)
     swaps = []
@@ -179,7 +200,7 @@
         group = (1 - place.x) if t == 0 else place.x
         src = partial.at[group * 2 + 1 - place.core]
         swaps.append(send(src, swap.at[t], gs, gr, t, place.partner()))
-    ring = Ring(place, block, whole, ring_part)
+    ring = Rings(place, block, whole, ring_part)
     ring.start()
 
     def add(first, second, out):
@@ -196,7 +217,7 @@
     over = send(ours, cross, gs, gr, 2, place.across())
     swaps[1].wait_recv()
     own = partial.at[place.x * 2 + place.core]
-    mid = ring.forward // 2
+    mid = ring.steps // 2
     for s in range(1, mid + 1):
         ring.step(s)
     over.wait_recv()
@@ -216,7 +237,7 @@
     for step in range(1, chips):
         chip = (place.chip + step) % chips
         back.append(send(total.at[chip], returned.at[place.chip], rs, rr, step, place.peer(chip)))
-    for s in range(mid + 1, ring.forward + 1):
+    for s in range(mid + 1, ring.steps + 1):
         ring.step(s)
     ring.finish()
     local.wait()
@@ -252,7 +273,7 @@
         ],
         in_specs=[vmem] * 3,
         out_specs=[hbm] * 3,
-        scratch_shapes=ring_sems(chips)
+        scratch_shapes=ring_sems(chips, pieces_of(rows))
         + [dma((chips,)), dma((chips,)), dma((4,)), dma((4,)), dma],
         compiler_params=pltpu.CompilerParams(collective_id=1, has_side_effects=True),
         name="gather_up_and_dispatch",
@@ -277,7 +298,7 @@
             pltpu.VMEM((chips, capacity, width), bf16),
             pltpu.VMEM((chips, capacity, width), bf16),
         ]
-        + ring_sems(chips)
+        + ring_sems(chips, pieces_of(rows))
         + [dma((chips,)), dma((chips,)), dma((3,)), dma((3,)), dma],
         compiler_params=pltpu.CompilerParams(
             collective_id=2, has_side_effects=True, vmem_limit_bytes=60 * 1024 * 1024

time: 229 us -> 214 us (0.934)
  Pallas kernels: 176 us -> 161 us
    pallas_call x1, Pallas kernels: 90.7 us -> 81.7 us  [on_device(): pl.pallas_call(functools.partial(second_kernel, chips), out_shape=[jax.Sh...]
    pallas_call x1, Pallas kernels: 85.7 us -> 79 us  [on_device(): pl.pallas_call(functools.partial(first_kernel, chips), out_shape=[jax.Sha...]
where the time goes in v2:
time: 214 us; the launch traced here: 212 us
  Pallas kernels  161 us (75%)
  matrix products  32.3 us (15%)
  waiting for transfers between devices  14.9 us (7%)
  other arithmetic  2.4 us (1%)
    pallas_call x1, Pallas kernels, on_device(): pl.pallas_call(functools.partial(second_kernel, chips), out_shape=[jax.Sh...  81.7 us
    pallas_call x1, Pallas kernels, on_device(): pl.pallas_call(functools.partial(first_kernel, chips), out_shape=[jax.Sha...  79 us
    ppermute x1, waiting for transfers between devices, on_device(): lax.ppermute(shared_part[tok_rows:].astype(bf16), 'tensor', [(0, 1), (1,...  14.9 us
    dot_general x1, matrix products, on_device(): jnp.dot(hidden, routed_down[0], preferred_element_type=jnp.float32)  14.5 us
    dot_general x1, matrix products, on_device(): lax.dot_general(shared_hidden, down.reshape(n_expert * rows, part), (((1,...  12.9 us
  transfers between devices with their start and end apart: 1, of which 1 were waited for; matrix products, arithmetic and copies ran while one was open for 0% of the time, Pallas kernels for 0%

profile of v2, /device:TPU:13, one launch (start us, length us, event | category | flops | bytes accessed | tf_op | source)
XLA Modules:
  0.0 211.8 jit_solution(6523531974655030694)
XLA Ops:
  0.0 0.7 fusion.21
  0.7 0.2 reduce_window_sum.11
  0.9 0.8 select_reduce_fusion
  1.7 0.7 multiply_add_fusion
  2.4 2.4 %convolution_convert_fusion = bf16[192,2560]{1,0:T(8,128)(2,1)} fusion(bf16[128,2560]{1,0:T(8,128)(2,1)} %tokens.1, s32[128]{0:T(128)S(1)} %multiply_add_fusion), kind=kOutput, calls=%fused_computation.5 | convolution fusion | flops 126345216 | bytes 1638912 | tf_op jit(solution)/shard_map/dot_general | solution.py:266
  4.9 79.0 %gather_up_and_dispatch.1 = (bf16[4,8,24,2560]{3,2,1,0:T(8,128)(2,1)}, bf16[128,2560]{1,0:T(8,128)(2,1)}, bf16[16,160,2048]{2,1,0:T(8,128)(2,1)}) custom-call(bf16[8,24,2560]{2,1,0:T(8,128)(2,1)} %bitcast.30, bf16[128,2560]{1,0:T(8,128)(2,1)} %tokens.1, bf16[160,2048]{1,0:T(8,128)(2,1)} %block.1), custom_call_target="tpu_custom_call" | custom-call | tf_op jit(solution)/shard_map/gather_up_and_dispatch/pallas_call | solution.py:267
  83.9 14.5 %fusion.4 = bf16[768,2560]{1,0:T(8,128)(2,1)} fusion(bf16[1,1024,2560]{2,1,0:T(8,128)(2,1)} %param.11, bf16[768,2560]{1,0:T(8,128)(2,1)} %bitcast.37, bf16[1,2560,1024]{2,1,0:T(8,128)(2,1)} %param.10), kind=kOutput, calls=%fused_computation.4 | convolution fusion | flops 8058961920 | bytes 18350080 | tf_op jit(solution)/shard_map/dot_general | solution.py:286
  98.4 0.0 copy-start
  98.4 81.7 %gather_down_and_return.1 = (bf16[8,24,2560]{2,1,0:T(8,128)(2,1)}, bf16[16,160,2048]{2,1,0:T(8,128)(2,1)}) custom-call(bf16[4,8,24,2560]{3,2,1,0:T(8,128)(2,1)} %bitcast.29, bf16[160,2048]{1,0:T(8,128)(2,1)} %bitcast.32), custom_call_target="tpu_custom_call" | custom-call | tf_op jit(solution)/shard_map/gather_down_and_return/pallas_call | solution.py:287
  180.1 0.0 copy-done
  180.1 0.0 copy-start.1
  180.1 12.9 %fusion.19 = f32[256,2560]{1,0:T(8,128)S(1)} fusion(bf16[2560,2048]{1,0:T(8,128)(2,1)} %bitcast.36, bf16[2560,2048]{1,0:T(8,128)(2,1)} %bitcast.35, bf16[128,2560]{1,0:T(8,128)(2,1)} %get-tuple-element.12, bf16[128,2560]{1,0:T(8,128)(2,1)S(1)} %copy-done), kind=kOutput, calls=%fused_computation.16 | convolution fusion | flops 5373952000 | bytes 24903680 | tf_op jit(solution)/shard_map/dot_general | solution.py:312
  193.0 0.1 slice.15
  193.1 1.3 collective-permute-start
  194.4 0.0 copy-done.1
  194.4 14.9 %collective-permute-done = bf16[128,2560]{1,0:T(8,128)(2,1)S(1)} collective-permute-done((bf16[128,2560]{1,0:T(8,128)(2,1)S(1)}, bf16[128,2560]{1,0:T(8,128)(2,1)S(1)}, u32[]{:S(2)}, u32[]{:S(2)}) %collective-permute-start) | collective-permute-done | bytes 655392 | tf_op jit(solution)/shard_map/ppermute | solution.py:318
  209.3 2.5 %add_convert_fusion = bf16[128,2560]{1,0:T(8,128)(2,1)} fusion(bf16[128,2560]{1,0:T(8,128)(2,1)S(1)} %collective-permute-done, f32[256,2560]{1,0:T(8,128)S(1)} %fusion.19, bf16[192,2560]{1,0:T(8,128)(2,1)} %bitcast.31, f32[128]{0:T(128)S(1)} %bitcast_convert_fusion, s32[128]{0:T(128)S(1)} %multiply_add_fusion), kind=kOutput, calls=%fused_computation.15 | convolution fusion | flops 127492096 | bytes 3605504 | tf_op jit(solution)/shard_map/st,sd->td/dot_general | solution.py:319
  (1 shorter events, 0.0 us)
Async XLA Ops:
  98.4 81.7 %copy-start = (bf16[128,2560]{1,0:T(8,128)(2,1)S(1)}, bf16[128,2560]{1,0:T(8,128)(2,1)}, u32[]{:S(2)}) copy-start(bf16[128,2560]{1,0:T(8,128)(2,1)} %tokens.1) | copy-start | bytes 1966084
  180.1 14.2 %copy-start.1 = (bf16[128,1]{0,1:T(2,128)(2,1)S(1)}, bf16[128,1]{0,1:T(2,128)(2,1)}, u32[]{:S(2)}) copy-start(bf16[128,1]{0,1:T(2,128)(2,1)} %param.9) | copy-start | bytes 772
  193.1 16.2 %collective-permute-start = (bf16[128,2560]{1,0:T(8,128)(2,1)S(1)}, bf16[128,2560]{1,0:T(8,128)(2,1)S(1)}, u32[]{:S(2)}, u32[]{:S(2)}) collective-permute-start(bf16[128,2560]{1,0:T(8,128)(2,1)S(1)} %slice.15), channel_id=1, source_target_pairs={{0,1},{1,0},{2,3},{3,2},{4,5},{5,4},{6,7},{7,6},{8,9},{9,8},{10,11... | collective-permute-start | bytes 1966088 | tf_op jit(solution)/shard_map/ppermute | solution.py:318
